TPU v7x, 32 devices: a whole 2x2x4 slice. The times are simulated.
32 devices in a mesh: ep: 16 (over z, x, core), dp: 2 (over y).
Axes of the slice: x: 2, y: 2, z: 4, core: 2. Of those that a mesh axis runs over, the one named last changes fastest.
Arguments:
- tokens: bfloat16 [4096, 2048], P(('dp', 'ep')), parts along dimension 0, may hold values from -6 to 6
- expert_ids: int32 [4096, 8], P(('dp', 'ep')), parts along dimension 0, may hold values from 0 to 15, all different within a row; in each aligned block of 128 rows (0 to 127, 128 to 255, ...) at most 96 rows name the same one
- route_logits: float32 [4096, 8], P(('dp', 'ep')), parts along dimension 0, may hold values from -3 to 300
- w_gate: bfloat16 [16, 2048, 1024], P('ep'), may hold values from -0.125 to 0.125
- w_up: bfloat16 [16, 2048, 1024], P('ep'), may hold values from -0.125 to 0.125
- w_down: bfloat16 [16, 1024, 2048], P('ep'), may hold values from -0.1875 to 0.1875
Outputs:
- mixed_rows: bfloat16 [4096, 2048], P(('dp', 'ep')), parts along dimension 0
There are 2 independent parts, one for each index of `dp`. A program takes and returns all parts, laid end to end along the dimension named above; an argument that names none is the same for every part. Nothing has to cross between parts.
Inputs may be any that keep to these rules, and one draw needn't show every extreme that they name: `expert_ids`: each row names 8 different experts; among the 128 rows of one device no expert is named more than 96 times, a bound that some block reaches.
All inputs are finite; a program needn't handle non-finite values.
Results may differ from a plain program's by a relative error of at most 0.0058.
Values may be sent and summed in bfloat16 or wider, within the bound.
A program may use at most 128 MiB of HBM per device.

v0:
```python
import functools

import jax
import jax.numpy as jnp
from jax import lax
from jax.experimental import pallas as pl
from jax.experimental.pallas import tpu as pltpu
from jax.sharding import PartitionSpec as P

VMEM_BYTES = 63 * 1024 * 1024


def expert_ffn(rows, gate_weight, up_weight, down_weight):
    gate = jnp.dot(rows, gate_weight, preferred_element_type=jnp.float32)
    up_part = jnp.dot(rows, up_weight, preferred_element_type=jnp.float32)
    hidden = (jax.nn.silu(gate) * up_part).astype(jnp.bfloat16)
    return jnp.dot(hidden, down_weight, preferred_element_type=jnp.float32).astype(jnp.bfloat16)


def blockwise(rows, live_rows, weights):
    turns = (live_rows + 127) // 128

    def step(block_index, result):
        first_row = block_index * 128
        block_rows = lax.dynamic_slice_in_dim(rows, first_row, 128, 0)
        answer = expert_ffn(block_rows, weights[0], weights[1], weights[2])
        return lax.dynamic_update_slice_in_dim(result, answer, first_row, 0)

    return lax.fori_loop(jnp.int32(0), turns, step, jnp.zeros(rows.shape, jnp.bfloat16))


def per_device(tokens, expert_ids, route_logits, w_gate, w_up, w_down):
    tok_rows, model_width = tokens.shape
    picks = expert_ids.shape[1]
    experts = lax.axis_size("ep")
    capacity = min(tok_rows, 3 * tok_rows * picks // (2 * experts))
    row_quota = tok_rows * picks
    received = experts * capacity
    spill_count = (max(received - row_quota, 128) + 127) // 128 * 128
    length = row_quota + spill_count
    flat_ids = expert_ids.reshape(-1)
    one_hot = (flat_ids[:, None] == jnp.arange(experts, dtype=jnp.int32)[None, :]).astype(jnp.int32)
    earlier = jnp.cumsum(one_hot, axis=0) - one_hot
    slot_rank = jnp.sum(earlier * one_hot, axis=1)
    counts = jnp.sum(one_hot, axis=0)
    slot_place = flat_ids * capacity + slot_rank
    source_row = jnp.arange(row_quota, dtype=jnp.int32) // picks
    slot_token = jnp.full((received,), tok_rows, jnp.int32).at[slot_place].set(source_row)
    padded_tokens = jnp.concatenate([tokens, jnp.zeros((1, model_width), tokens.dtype)], 0)
    outgoing = padded_tokens[slot_token].reshape(experts, capacity, model_width)
    all_counts = lax.all_gather(counts, "ep", axis=0, tiled=True).reshape(experts, experts)
    own_index = lax.axis_index("ep")
    from_sources = lax.dynamic_index_in_dim(all_counts, own_index, 1, keepdims=False)
    incoming = lax.all_to_all(outgoing, "ep", split_axis=0, concat_axis=0, tiled=True)
    offsets = jnp.cumsum(from_sources) - from_sources
    live_rows = jnp.sum(from_sources)
    slot_numbers = jnp.arange(capacity, dtype=jnp.int32)
    live_slot = slot_numbers[None, :] < from_sources[:, None]
    position = jnp.where(live_slot, offsets[:, None] + slot_numbers[None, :], length).reshape(-1)
    gather_order = (
        jnp.full((length,), received, jnp.int32)
        .at[position]
        .set(jnp.arange(received, dtype=jnp.int32), mode="drop")
    )
    flat_incoming = jnp.concatenate(
        [incoming.reshape(received, model_width), jnp.zeros((1, model_width), jnp.bfloat16)], 0
    )
    packed = flat_incoming[gather_order]
    own_weights = (w_gate[0], w_up[0], w_down[0])
    results = blockwise(packed, live_rows, own_weights)
    results_ext = jnp.concatenate([results, jnp.zeros((1, model_width), jnp.bfloat16)], 0)
    outgoing_back = results_ext[position].reshape(experts, capacity, model_width)
    answers = lax.all_to_all(outgoing_back, "ep", split_axis=0, concat_axis=0, tiled=True)
    mix_weights = jax.nn.softmax(route_logits, axis=-1)
    picked = answers.reshape(received, model_width)[slot_place].reshape(
        tok_rows, picks, model_width
    )
    mixed_rows = jnp.zeros((tok_rows, model_width), jnp.float32)
    for column in range(picks):
        mixed_rows = mixed_rows + mix_weights[:, column : column + 1] * picked[:, column].astype(
            jnp.float32
        )
    return mixed_rows.astype(jnp.bfloat16)


def ring_place(chip, ring):
    column, row = chip % 2, chip // 2
    return row + column * (ring - 1 - 2 * row)


def chip_at(place, ring):
    column = place // (ring // 2)
    return 2 * (place + column * (ring - 1 - 2 * place)) + column


def remote(src, dst, send_sem, recv_sem, target):
    return pltpu.make_async_remote_copy(
        src_ref=src,
        dst_ref=dst,
        send_sem=send_sem,
        recv_sem=recv_sem,
        device_id={"ep": target},
        device_id_type=pl.DeviceIdType.MESH,
    )


def fused_kernel(
    n,
    tok_ref,
    ids_ref,
    logits_ref,
    wg_hbm,
    wu_hbm,
    wd_hbm,
    out_ref,
    xs,
    wg,
    wu,
    wd,
    ps,
    sib,
    got_r,
    got_l,
    put_r,
    put_l,
    hid,
    gate_rows,
    gate_all,
    gate_col,
    load_sem,
    gate_send,
    gate_recv,
    gate_out,
    gate_in,
    ag_send,
    ag_recv,
    pass_send,
    pass_recv,
    own_sem,
    sib_send,
    sib_recv,
    rs_send,
    rs_recv,
):
    ring = n // 2
    far = ring // 2
    chunks = ring - 1
    tok_rows, width = tok_ref.shape
    part = tok_rows // 2
    ff = wg.shape[1]
    me = lax.axis_index("ep")
    core, chip = me % 2, me // 2
    other = 1 - core
    place = ring_place(chip, ring)
    right = chip_at((place + 1) % ring, ring) * 2 + core
    left = chip_at((place + ring - 1) % ring, ring) * 2 + core
    twin = chip * 2 + other

    barrier = pltpu.get_barrier_semaphore()

    for friend in (right, left, twin):
        pl.semaphore_signal(
            barrier,
            inc=1,
            device_id={"ep": friend},
            device_id_type=pl.DeviceIdType.MESH,
        )

    own_load = pltpu.make_async_copy(tok_ref, xs.at[0, core], load_sem.at[0])
    own_load.start()
    weight_loads = [
        pltpu.make_async_copy(wg_hbm.at[0], wg, load_sem.at[1]),
        pltpu.make_async_copy(wu_hbm.at[0], wu, load_sem.at[2]),
        pltpu.make_async_copy(wd_hbm.at[0], wd, load_sem.at[3]),
    ]
    for load in weight_loads:
        load.start()

    logits = logits_ref[...]
    powers = jnp.exp(logits - jnp.max(logits, axis=0, keepdims=True))
    gates = powers / jnp.sum(powers, axis=0, keepdims=True)
    ids = ids_ref[...]
    for expert in range(n):
        gate_rows[core, expert] = jnp.sum(
            jnp.where(ids == expert, gates, 0.0), axis=0, keepdims=True
        )

    own_load.wait()
    pl.semaphore_wait(barrier, 3)

    def ag_copy(way, s):
        target = right if way == 0 else left
        rows = pl.ds(way * part, part)
        if s < 2:
            lane = s if way == 0 else 1 - s
            src = xs.at[0, core, pl.ds(lane * part, part)]
        else:
            src = xs.at[s - 1, core, rows]
        return remote(
            src, xs.at[s + 1, core, rows], ag_send.at[way, s], ag_recv.at[way, s], target
        )

    def pass_copy(way, s, whose):
        ref = xs.at[s + 1, whose, pl.ds(way * part, part)]
        return remote(ref, ref, pass_send.at[way, s], pass_recv.at[way, s], twin)

    def own_copy(whose):
        ref = xs.at[0, whose]
        return remote(ref, ref, own_sem.at[0], own_sem.at[1], twin)

    def own_gate(whose):
        ref = gate_rows.at[whose]
        return remote(ref, ref, own_sem.at[2], own_sem.at[3], twin)

    def gate_copy(way, hop):
        return remote(
            gate_rows.at[core] if hop == 1 else gate_all.at[way, hop - 2, core],
            gate_all.at[way, hop - 1, core],
            gate_send.at[way, hop - 1],
            gate_recv.at[way, hop - 1],
            right if way == 0 else left,
        )

    def gate_pass(way, hop, whose):
        ref = gate_all.at[way, hop - 1, whose]
        return remote(
            ref, ref, gate_out.at[way, hop - 1], gate_in.at[way, hop - 1], twin
        )

    for way in range(2):
        gate_copy(way, 1).start()
        ag_copy(way, 0).start()
    for way in range(2):
        ag_copy(way, 1).start()
    own_copy(core).start()
    own_gate(core).start()

    turns = list(range(chunks - 4)) + [chunks - 3, chunks - 4, chunks - 1, chunks - 2]
    waiting, seen = [s for s in turns if s >= 2], set()

    def ag_event(k):
        seen.add(k)
        ready = []
        while waiting and waiting[0] - 2 in seen:
            ready.append(waiting.pop(0))
        for way in range(2):
            hop = k // 2 + 1
            if k % 2 == 0:
                gate_copy(way, hop).wait_recv()
                if hop < far:
                    gate_copy(way, hop + 1).start()
            ag_copy(way, k).wait_recv()
            for s in ready:
                ag_copy(way, s).start()
            pass_copy(way, k, core).start()
            if k % 2 == 0:
                gate_pass(way, hop, core).start()

    def sib_copy(slot, whose):
        return remote(
            ps.at[slot, whose], sib.at[slot], sib_send.at[slot], sib_recv.at[slot], twin
        )

    def rs_copy(way, k):
        put, got, target = (put_r, got_r, right) if way == 0 else (put_l, got_l, left)
        return remote(
            put.at[k], got.at[k], rs_send.at[way, k], rs_recv.at[way, k], target
        )

    def chip_sum(slot, rows):
        return ps[slot, core, rows, :].astype(jnp.float32) + sib[slot, rows, :].astype(
            jnp.float32
        )

    def rs_event(k):
        sib_copy(k + 1, core).wait_recv()
        for way in range(2):
            put, got = (put_r, got_r) if way == 0 else (put_l, got_l)
            side = way if k == chunks - 1 else 1 - way
            total = chip_sum(k + 1, pl.ds(side * part, part))
            if k not in (chunks - 1, chunks - 3):
                before = chunks - 1 if k == chunks - 2 else k + 2
                rs_copy(way, before).wait_recv()
                total = total + got[before].astype(jnp.float32)
            put[k] = total.astype(jnp.bfloat16)
            rs_copy(way, k).start()

    def arrive(slot):
        if slot == 0:
            own_copy(other).wait_recv()
            own_gate(other).wait_recv()
        else:
            for way in range(2):
                pass_copy(way, slot - 1, other).wait_recv()
                if slot % 2 == 1:
                    gate_pass(way, (slot + 1) // 2, other).wait_recv()

    ff_tile = ff // 4
    out_tile = width // 4

    def hidden_part(slot, first, last):
        def body(j, carry):
            x = xs[slot].reshape(2 * tok_rows, width)
            cols = pl.ds(pl.multiple_of(j * ff_tile, ff_tile), ff_tile)
            gate = jnp.dot(x, wg[:, cols], preferred_element_type=jnp.float32)
            up = jnp.dot(x, wu[:, cols], preferred_element_type=jnp.float32)
            hid[:, cols] = (gate / (1.0 + jnp.exp(-gate)) * up).astype(jnp.bfloat16)
            return carry

        lax.fori_loop(first, last, body, 0)

    def answer_part(slot):
        def body(j, carry):
            cols = pl.ds(pl.multiple_of(j * out_tile, out_tile), out_tile)
            answer = jnp.dot(hid[...], wd[:, cols], preferred_element_type=jnp.float32)
            scale = jnp.concatenate([gate_col[...]] * (out_tile // 128), axis=1)
            ps[slot, :, :, cols] = (
                (answer * scale).astype(jnp.bfloat16).reshape(2, tok_rows, out_tile)
            )
            return carry

        lax.fori_loop(0, 4, body, 0)

    order = [0] + [k + 1 for k in range(chunks - 4)]
    order += [chunks - 2, chunks, chunks - 1, chunks - 3]
    last = 3 * ring
    hooks = {}
    times = [(5 * i + 1) // 2 + 1 for i in range(chunks - 4)]
    times += [last - 14, last - 12, last - 10, last - 7]
    for time, k in zip(times, turns):
        hooks.setdefault(time, []).append(functools.partial(ag_event, k))
    firsts, seconds = list(range(chunks - 3, -1, -2)), [chunks - 1]
    seconds += list(range(chunks - 2, 0, -2))
    sends = [k for pair in zip(firsts, seconds) for k in pair] + seconds[len(firsts) :]
    for third, k in zip((last - 10, last - 6, last - 5, last - 2), sends):
        hooks.setdefault(third, []).append(functools.partial(rs_event, k))

    third = 0
    for index, slot in enumerate(order):
        arrive(slot)
        if index == 0:
            weight_loads[0].wait()
            weight_loads[1].wait()
        for piece in range(3):
            if piece == 0:
                hidden_part(slot, 0, 2)
            elif piece == 1:
                hidden_part(slot, 2, 4)
            else:
                if index == 0:
                    weight_loads[2].wait()
                for way in range(2):
                    hop = (slot + 1) // 2
                    lane = (slot + 1 + way) % 2 if slot > 0 else way
                    for whose in range(2):
                        if hop == 0:
                            row = gate_rows[whose, me]
                        else:
                            row = gate_all[way, hop - 1, whose, me]
                        gate_col[pl.ds(whose * tok_rows + way * part, part), :] = (
                            jnp.broadcast_to(row, (128, tok_rows)).T[
                                lane * part : (lane + 1) * part
                            ]
                        )
                answer_part(slot)
                sib_copy(slot, other).start()
            for hook in hooks.get(third, []):
                hook()
            third += 1

    for k in sends[4:]:
        rs_event(k)
    sib_copy(0, core).wait_recv()
    for lane in (1, 0):
        rows = pl.ds(lane * part, part)
        total = chip_sum(0, rows)
        for way, got in ((0, got_r), (1, got_l)):
            k = 1 if lane == way else 0
            rs_copy(way, k).wait_recv()
            total = total + got[k].astype(jnp.float32)
        out_ref[rows, :] = total.astype(jnp.bfloat16)
    for s in range(chunks):
        for way in range(2):
            ag_copy(way, s).wait_send()
            pass_copy(way, s, core).wait_send()
            rs_copy(way, s).wait_send()
    for slot in range(ring):
        sib_copy(slot, other).wait_send()
    own_copy(core).wait_send()
    own_gate(core).wait_send()
    for hop in range(1, far + 1):
        for way in range(2):
            gate_copy(way, hop).wait_send()
            gate_pass(way, hop, core).wait_send()


def fused_scratch(n, tok_rows, width, ff):
    ring = n // 2
    chunks, part, bf16 = ring - 1, tok_rows // 2, jnp.bfloat16
    buffers = [
        ((ring, 2, tok_rows, width), bf16),
        ((width, ff), bf16),
        ((width, ff), bf16),
        ((ff, width), bf16),
        ((ring, 2, tok_rows, width), bf16),
        ((ring, tok_rows, width), bf16),
        ((chunks, part, width), bf16),
        ((chunks, part, width), bf16),
        ((chunks, part, width), bf16),
        ((chunks, part, width), bf16),
        ((2 * tok_rows, ff), bf16),
        ((2, n, 1, tok_rows), jnp.float32),
        ((2, ring // 2, 2, n, 1, tok_rows), jnp.float32),
        ((2 * tok_rows, 128), jnp.float32),
    ]
    hops, moves = (2, ring // 2), (2, chunks)
    sems = [(4,), hops, hops, hops, hops, moves, moves, moves, moves, (4,)]
    sems += [(ring,), (ring,), moves, moves]
    size = 0
    for shape, kind in buffers:
        count = jnp.dtype(kind).itemsize
        for extent in shape:
            count = count * extent
        size = size + count
    scratch = [pltpu.VMEM(shape, kind) for shape, kind in buffers]
    return scratch + [pltpu.SemaphoreType.DMA(shape) for shape in sems], size


def fused_device(tokens, expert_ids, route_logits, w_gate, w_up, w_down):
    n = lax.axis_size("ep")
    tok_rows, width = tokens.shape
    ff = w_gate.shape[2]
    scratch, size = fused_scratch(n, tok_rows, width, ff)
    anywhere, vmem = pl.BlockSpec(memory_space=pl.ANY), pl.BlockSpec(memory_space=pltpu.VMEM)
    return pl.pallas_call(
        functools.partial(fused_kernel, n),
        out_shape=jax.ShapeDtypeStruct((tok_rows, width), jnp.bfloat16),
        in_specs=[anywhere, vmem, vmem, anywhere, anywhere, anywhere],
        out_specs=vmem,
        scratch_shapes=scratch,
        compiler_params=pltpu.CompilerParams(
            collective_id=0, has_side_effects=True, vmem_limit_bytes=VMEM_BYTES
        ),
    )(tokens, expert_ids.T, route_logits.T, w_gate, w_up, w_down)


def layer(tokens, expert_ids, route_logits, w_gate, w_up, w_down):
    n = lax.axis_size("ep")
    tok_rows, width = tokens.shape
    ff = w_gate.shape[2]
    size = fused_scratch(n, tok_rows, width, ff)[1]
    fits = size + 8 * tok_rows * width < VMEM_BYTES
    if fits and n % 4 == 0 and n >= 16 and tok_rows == 128 and n <= 128:
        return fused_device(tokens, expert_ids, route_logits, w_gate, w_up, w_down)
    return per_device(tokens, expert_ids, route_logits, w_gate, w_up, w_down)


def solution(mesh):
    in_specs = (
        P(("dp", "ep"), None),
        P(("dp", "ep"), None),
        P(("dp", "ep"), None),
        P("ep", None, None),
        P("ep", None, None),
        P("ep", None, None),
    )
    out_specs = P(("dp", "ep"), None)
    return jax.shard_map(
        layer, mesh=mesh, in_specs=in_specs, out_specs=out_specs, check_vma=False
    )
```

profile of v0, /device:TPU:0, one launch (start us, length us, event | category | flops | bytes accessed | tf_op | source)
XLA Modules:
  0.0 93.5 jit_solution(17720232057798475105)
XLA Ops:
  0.0 91.7 %shard_map.64 = bf16[128,2048]{1,0:T(8,128)(2,1)} custom-call(bf16[128,2048]{1,0:T(8,128)(2,1)} %tok_ref.1, s32[8,128]{1,0:T(8,128)} %bitcast.2, f32[8,128]{1,0:T(8,128)} %bitcast.3, bf16[1,2048,1024]{2,1,0:T(8,128)(2,1)} %wg_hbm.1, bf16[1,2048,1024]{2,1,0:T(8,128)(2,1)} %wu_hbm.1, bf16[1,1024,2048]{2,1,0:T(8,128)(2,1)} %wd_hbm.1), custom_call_target="tpu_custom_call" | custom-call | tf_op jit(solution)/shard_map/pallas_call | solution.py:435
  91.7 1.9 %copy.8 = bf16[128,2048]{1,0:T(8,128)(2,1)} copy(bf16[128,2048]{1,0:T(8,128)(2,1)} %shard_map.64) | data formatting | bytes 1048576
where the time goes:
time: 93.7 us; the launch traced here: 93.5 us
  Pallas kernels  91.7 us (98%)
  local copies, waits for them, and re-layouts  1.88 us (2%)
    pallas_call x1, Pallas kernels, fused_device(): pl.pallas_call(functools.partial(fused_kernel, n), out_shape=jax.ShapeDty...  91.7 us
    unnamed x1, local copies, waits for them, and re-layouts  1.88 us

commit v1 on v0

v1 whole, which is shorter than its diff:
```python
import functools

import jax
import jax.numpy as jnp
from jax import lax
from jax.experimental import pallas as pl
from jax.experimental.pallas import tpu as pltpu
from jax.sharding import PartitionSpec as P

VMEM_BYTES = 63 * 1024 * 1024

KINDS = (1, 0, 0, 1, 0, 1, 0, 0)
END_BATCHES = (
    5, 2, 0, 3, 0, 0, 0, 1, 3, 2, 7, 7, 4, 6, 2, 3,
    7, 5, 3, 6, 1, 0, 1, 1, 6, 7, 6, 7, 6, 6, 2, 5,
    4, 3, 1, 0, 0, 1, 3, 3, 0, 4, 2, 4, 4, 4, 1, 5,
    5, 3, 2, 7, 7, 6, 5, 4, 1, 4, 5, 5, 7, 6, 2, 2,
)
MID_BATCHES = (
    6, 6, 0, 0, 0, 1, 4, 4, 0, 2, 5, 2, 1, 2, 7, 0,
    3, 7, 3, 1, 3, 0, 6, 6, 6, 4, 5, 5, 1, 3, 4, 6,
    7, 1, 6, 1, 4, 2, 5, 3, 7, 5, 2, 3, 3, 2, 0, 5,
    7, 4, 5, 4, 1, 4, 2, 2, 7, 6, 7, 5, 1, 3, 7, 0,
)
END_ORDER = (
    400, 200, 0, 600, 10, 401, 700, 201, 500, 1, 410, 601, 100, 701, 20, 300,
    420, 501, 411, 220, 101, 11, 210, 301, 430, 30, 421, 610, 221, 230, 21, 211,
    1000, 530, 431, 1010, 1020, 730, 611, 1030, 31, 231, 1040, 1050, 130, 1100, 1110, 330,
    1120, 2030, 2221, 2021, 731, 2411, 510, 1130, 1140, 630, 131, 2020, 1150, 2010, 1200, 110,
    1210, 1220, 511, 2530, 2421, 1230, 520, 2231, 2031, 1240, 631, 2410, 1250, 120, 1300, 111,
    710, 2220, 1310, 1320, 521, 2101, 2330, 1330, 2230, 2731, 531, 1340, 1350, 310, 121, 2420,
    1400, 711, 2510, 1410, 331, 2131, 2431, 1420, 2011, 1430, 720, 2730, 1440, 1450, 620, 1500,
    311, 2130, 2401, 1510, 320, 2521, 1520, 2430, 2631, 1530, 721, 2601, 321, 1540, 2511, 1550,
    621, 2701, 2520, 2531, 2711, 1600, 2201, 1610, 2331, 1620, 2630, 1630, 1640, 1650, 2001, 2710,
    1700, 1710, 2321, 2121, 2320, 2721, 1720, 1730, 2310, 2621, 1740, 2000, 2211, 1750, 2400, 2120,
    2311, 2111, 2720, 2611, 2620, 2501, 2210, 2301, 2110, 2600, 2610, 2500, 2200, 2300, 2700, 2100,
)
MID_ORDER = (
    0, 400, 200, 600, 430, 10, 401, 410, 30, 201, 230, 601, 210, 1, 431, 420,
    411, 530, 730, 20, 231, 220, 31, 211, 11, 130, 421, 520, 330, 731, 630, 720,
    221, 21, 531, 131, 120, 331, 631, 320, 721, 500, 121, 620, 100, 1000, 501, 1010,
    621, 510, 1020, 1030, 101, 110, 1040, 1050, 700, 1100, 1110, 511, 1120, 2221, 111, 2731,
    521, 2011, 2020, 1130, 1140, 701, 300, 1150, 2131, 1200, 321, 2010, 1210, 710, 1220, 2021,
    1230, 610, 1240, 2401, 1250, 301, 1300, 310, 2411, 1310, 711, 2320, 1320, 2121, 1330, 611,
    2111, 1340, 311, 1350, 2631, 1400, 1410, 2421, 1420, 2520, 2721, 2220, 1430, 1440, 2431, 1450,
    2120, 1500, 2101, 1510, 2031, 2030, 2511, 2611, 1520, 2420, 1530, 2530, 2720, 2621, 1540, 2330,
    2211, 1550, 2510, 2601, 1600, 2521, 1610, 2711, 2430, 1620, 2321, 2501, 1630, 2620, 1640, 2210,
    1650, 1700, 2531, 1710, 2311, 2231, 2331, 2410, 2001, 1720, 1730, 2310, 2630, 2701, 1740, 1750,
    2110, 2230, 2301, 2000, 2500, 2730, 2201, 2130, 2400, 2710, 2610, 2300, 2200, 2700, 2100, 2600,
)
ORDERS = (END_ORDER, MID_ORDER)


def expert_ffn(rows, gate_weight, up_weight, down_weight):
    gate = jnp.dot(rows, gate_weight, preferred_element_type=jnp.float32)
    up_part = jnp.dot(rows, up_weight, preferred_element_type=jnp.float32)
    hidden = (jax.nn.silu(gate) * up_part).astype(jnp.bfloat16)
    return jnp.dot(hidden, down_weight, preferred_element_type=jnp.float32).astype(jnp.bfloat16)


def blockwise(rows, live_rows, weights):
    turns = (live_rows + 127) // 128

    def step(block_index, result):
        first_row = block_index * 128
        block_rows = lax.dynamic_slice_in_dim(rows, first_row, 128, 0)
        answer = expert_ffn(block_rows, weights[0], weights[1], weights[2])
        return lax.dynamic_update_slice_in_dim(result, answer, first_row, 0)

    return lax.fori_loop(jnp.int32(0), turns, step, jnp.zeros(rows.shape, jnp.bfloat16))


def per_device(tokens, expert_ids, route_logits, w_gate, w_up, w_down):
    tok_rows, model_width = tokens.shape
    picks = expert_ids.shape[1]
    experts = lax.axis_size("ep")
    capacity = min(tok_rows, 3 * tok_rows * picks // (2 * experts))
    row_quota = tok_rows * picks
    received = experts * capacity
    spill_count = (max(received - row_quota, 128) + 127) // 128 * 128
    length = row_quota + spill_count
    flat_ids = expert_ids.reshape(-1)
    one_hot = (flat_ids[:, None] == jnp.arange(experts, dtype=jnp.int32)[None, :]).astype(jnp.int32)
    earlier = jnp.cumsum(one_hot, axis=0) - one_hot
    slot_rank = jnp.sum(earlier * one_hot, axis=1)
    counts = jnp.sum(one_hot, axis=0)
    slot_place = flat_ids * capacity + slot_rank
    source_row = jnp.arange(row_quota, dtype=jnp.int32) // picks
    slot_token = jnp.full((received,), tok_rows, jnp.int32).at[slot_place].set(source_row)
    padded_tokens = jnp.concatenate([tokens, jnp.zeros((1, model_width), tokens.dtype)], 0)
    outgoing = padded_tokens[slot_token].reshape(experts, capacity, model_width)
    all_counts = lax.all_gather(counts, "ep", axis=0, tiled=True).reshape(experts, experts)
    own_index = lax.axis_index("ep")
    from_sources = lax.dynamic_index_in_dim(all_counts, own_index, 1, keepdims=False)
    incoming = lax.all_to_all(outgoing, "ep", split_axis=0, concat_axis=0, tiled=True)
    offsets = jnp.cumsum(from_sources) - from_sources
    live_rows = jnp.sum(from_sources)
    slot_numbers = jnp.arange(capacity, dtype=jnp.int32)
    live_slot = slot_numbers[None, :] < from_sources[:, None]
    position = jnp.where(live_slot, offsets[:, None] + slot_numbers[None, :], length).reshape(-1)
    gather_order = (
        jnp.full((length,), received, jnp.int32)
        .at[position]
        .set(jnp.arange(received, dtype=jnp.int32), mode="drop")
    )
    flat_incoming = jnp.concatenate(
        [incoming.reshape(received, model_width), jnp.zeros((1, model_width), jnp.bfloat16)], 0
    )
    packed = flat_incoming[gather_order]
    own_weights = (w_gate[0], w_up[0], w_down[0])
    results = blockwise(packed, live_rows, own_weights)
    results_ext = jnp.concatenate([results, jnp.zeros((1, model_width), jnp.bfloat16)], 0)
    outgoing_back = results_ext[position].reshape(experts, capacity, model_width)
    answers = lax.all_to_all(outgoing_back, "ep", split_axis=0, concat_axis=0, tiled=True)
    mix_weights = jax.nn.softmax(route_logits, axis=-1)
    picked = answers.reshape(received, model_width)[slot_place].reshape(
        tok_rows, picks, model_width
    )
    mixed_rows = jnp.zeros((tok_rows, model_width), jnp.float32)
    for column in range(picks):
        mixed_rows = mixed_rows + mix_weights[:, column : column + 1] * picked[:, column].astype(
            jnp.float32
        )
    return mixed_rows.astype(jnp.bfloat16)


def remote(src, dst, send_sem, recv_sem, target):
    return pltpu.make_async_remote_copy(
        src_ref=src,
        dst_ref=dst,
        send_sem=send_sem,
        recv_sem=recv_sem,
        device_id={"ep": target},
        device_id_type=pl.DeviceIdType.MESH,
    )


PIECES = len(KINDS)
CELLS = [(p, d, c) for p in range(PIECES) for d in range(4) for c in range(2)]
PARTS = 6


def slots_of(batches):
    filled, table = [0] * PIECES, {}
    for cell, batch in zip(CELLS, batches):
        table[cell] = (batch, filled[batch])
        filled[batch] += 1
    return table


SLOT = (slots_of(END_BATCHES), slots_of(MID_BATCHES))


def at(cell):
    return (cell[0] * 4 + cell[1]) * 2 + cell[2]


def place_of(cell):
    return cell[1] * 2 + cell[2]


def moves(role, cell):
    p, d, c = cell
    first_z = KINDS[p] == 0
    out = []
    if d == 0 and (c == 0 or not first_z):
        if role == 0:
            out.append(("in", 1, (p, 3, c)))
        else:
            out.append(("out", 0, (p, 1, c)))
            out.append(("in", 1, (p, 1, c)))
    elif d > 0 and (c == 0 or not first_z) and role == 1:
        if d == 3:
            out.append(("in", 1, (p, 2, c)))
        else:
            out.append(("out", 0, (p, d + 1, c)))
    if c == 0 and (first_z or d == 0):
        across = ("x", role, (p, d, 1))
        out = out + [across] if first_z else [across] + out
    return out


def fused_kernel(
    n,
    tok_ref,
    ids_ref,
    logits_ref,
    wg_hbm,
    wu_hbm,
    wd_hbm,
    out_ref,
    xs,
    wg,
    wu,
    wd,
    ps,
    sib,
    put,
    got_x,
    got_in,
    got_out,
    hid,
    gates,
    gate_tok,
    gate_col,
    load_sem,
    tok_sem,
    ag_send,
    ag_recv,
    twin_send,
    twin_recv,
    gate_send,
    gate_recv,
    gate_pass,
    sib_send,
    sib_recv,
    rs_send,
    x_recv,
    in_recv,
    out_recv,
):
    tok_rows, width = tok_ref.shape
    rows = tok_rows // PIECES
    ff = wg.shape[1]
    me = lax.axis_index("ep")
    core, chip = me % 2, me // 2
    other = 1 - core
    x, z = chip % 2, chip // 2
    depth = n // 4
    inward = jnp.where(z < depth // 2, 1, -1)
    at_end = jnp.logical_or(z == 0, z == depth - 1)
    at_mid = jnp.logical_not(at_end)
    peers = {
        "in": ((z + inward) * 2 + x) * 2 + core,
        "out": ((z - inward) * 2 + x) * 2 + core,
        "x": (z * 2 + 1 - x) * 2 + core,
        "twin": chip * 2 + other,
    }

    def by_role(end_part, mid_part):
        if end_part is not None:
            pl.when(at_end)(end_part)
        if mid_part is not None:
            pl.when(at_mid)(mid_part)

    barrier = pltpu.get_barrier_semaphore()

    def greet(friend):
        pl.semaphore_signal(
            barrier,
            inc=1,
            device_id={"ep": peers[friend]},
            device_id_type=pl.DeviceIdType.MESH,
        )

    greet("twin")
    greet("x")
    greet("in")
    by_role(None, lambda: greet("out"))

    def chunk(role, cell, whose):
        batch, place = SLOT[role][cell]
        return xs.at[(batch * PIECES + place) * 2 + whose]

    def own_load(role, p):
        return pltpu.make_async_copy(
            tok_ref.at[pl.ds(p * rows, rows)], chunk(role, (p, 0, 0), core), tok_sem.at[p]
        )

    def load_all(role):
        for code in ORDERS[role]:
            if code // 1000 == 0 and code % 100 == 0:
                own_load(role, code // 100).start()

    by_role(lambda: load_all(0), lambda: load_all(1))
    weight_loads = [
        pltpu.make_async_copy(wg_hbm.at[0], wg, load_sem.at[0]),
        pltpu.make_async_copy(wu_hbm.at[0], wu, load_sem.at[1]),
        pltpu.make_async_copy(wd_hbm.at[0], wd, load_sem.at[2]),
    ]
    for load in weight_loads:
        load.start()

    logits = logits_ref[...]
    powers = jnp.exp(logits - jnp.max(logits, axis=0, keepdims=True))
    shares = powers / jnp.sum(powers, axis=0, keepdims=True)
    ids = ids_ref[...]
    for expert in range(n):
        gates[core, expert] = jnp.sum(
            jnp.where(ids == expert, shares, 0.0), axis=0, keepdims=True
        )

    by_role(lambda: pl.semaphore_wait(barrier, 3), lambda: pl.semaphore_wait(barrier, 4))

    def ag_copy(role, cell, link, to_role, to_cell):
        return remote(
            chunk(role, cell, core),
            chunk(to_role, to_cell, core),
            ag_send.at[0],
            ag_recv.at[at(to_cell)],
            peers[link],
        )

    def pass_copy(role, cell, whose):
        batch, place = SLOT[role][cell]
        ref = chunk(role, cell, whose)
        return remote(ref, ref, twin_send.at[0], twin_recv.at[batch], peers["twin"])

    def gate_copy(cell, link, to_cell):
        return remote(
            gates.at[place_of(cell) * 2 + core],
            gates.at[place_of(to_cell) * 2 + core],
            gate_send.at[0],
            gate_recv.at[place_of(to_cell)],
            peers[link],
        )

    def gate_twin(cell, whose):
        place = place_of(cell)
        ref = gates.at[place * 2 + whose]
        return remote(ref, ref, gate_send.at[1], gate_pass.at[place], peers["twin"])

    def receive(role, cell):
        p, d, c = cell
        lead = p == 0
        if (d, c) == (0, 0):
            own_load(role, p).wait()
        else:
            if lead:
                gate_copy(cell, "x", cell).wait_recv()
            ag_copy(role, cell, "x", role, cell).wait_recv()
        for link, to_role, to_cell in moves(role, cell):
            if lead:
                gate_copy(cell, link, to_cell).start()
            ag_copy(role, cell, link, to_role, to_cell).start()
        if lead:
            gate_twin(cell, core).start()
        pass_copy(role, cell, core).start()

    def sib_copy(batch, half, whose):
        cols = pl.ds(half * (width // 2), width // 2)
        return remote(
            ps.at[batch, :, whose, :, cols],
            sib.at[batch, :, :, cols],
            sib_send.at[0],
            sib_recv.at[batch],
            peers["twin"],
        )

    sib_seen = (set(), set())
    put_used = [0, 0]

    def send_back(role, cell):
        p, d, c = cell
        first_z = KINDS[p] == 0
        batch, place = SLOT[role][cell]
        if batch not in sib_seen[role]:
            sib_seen[role].add(batch)
            ref = sib.at[batch]
            remote(ref, ref, sib_send.at[0], sib_recv.at[batch], peers["twin"]).wait_recv()
        total = ps[batch, place, core].astype(jnp.float32) + sib[batch, place].astype(jnp.float32)
        inbox = []
        if c == 0 and (first_z or d == 0):
            inbox.append((got_x, x_recv, p * 4 + d))
        if c == 0 or not first_z:
            if d == 0 or (d == 3 and role == 1):
                inbox.append((got_in, in_recv, (p * 2 + d // 3) * 2 + c))
            if role == 1 and d < 3:
                inbox.append((got_out, out_recv, (p * 3 + d) * 2 + c))
        for buffer, sem, index in inbox:
            ref = buffer.at[index]
            remote(ref, ref, rs_send.at[0], sem.at[index], peers["x"]).wait_recv()
            total = total + buffer[index].astype(jnp.float32)
        total = total.astype(jnp.bfloat16)
        if c == 1 and (first_z or d == 0):
            link, buffer, sem, index = "x", got_x, x_recv, p * 4 + d
        elif d == 0:
            out_ref[pl.ds(p * rows, rows), :] = total
            return
        elif role == 0:
            link, buffer, sem, index = "in", got_out, out_recv, (p * 3 + d - 1) * 2 + c
        elif d == 3:
            link, buffer, sem, index = "out", got_in, in_recv, p * 4 + c
        else:
            link, buffer, sem, index = "in", got_in, in_recv, (p * 2 + d - 1) * 2 + c
        slot = put_used[role]
        put_used[role] += 1
        put[slot] = total
        remote(put.at[slot], buffer.at[index], rs_send.at[0], sem.at[index], peers[link]).start()

    ff_tile = ff // 4
    out_tile = width // 4

    def hidden_part(batch, first, last):
        def body(j, carry):
            rows_in = xs[pl.ds(batch * 2 * PIECES, 2 * PIECES)].reshape(2 * tok_rows, width)
            cols = pl.ds(pl.multiple_of(j * ff_tile, ff_tile), ff_tile)
            gate = jnp.dot(rows_in, wg[:, cols], preferred_element_type=jnp.float32)
            up = jnp.dot(rows_in, wu[:, cols], preferred_element_type=jnp.float32)
            hid[:, cols] = (gate / (1.0 + jnp.exp(-gate)) * up).astype(jnp.bfloat16)
            return carry

        lax.fori_loop(first, last, body, 0)

    def answer_part(batch, first, last):
        def body(j, carry):
            cols = pl.ds(pl.multiple_of(j * out_tile, out_tile), out_tile)
            answer = jnp.dot(hid[...], wd[:, cols], preferred_element_type=jnp.float32)
            scale = jnp.concatenate([gate_col[...]] * (out_tile // 128), axis=1)
            ps[batch, :, :, :, cols] = (
                (answer * scale).astype(jnp.bfloat16).reshape(PIECES, 2, rows, out_tile)
            )
            return carry

        lax.fori_loop(first, last, body, 0)

    gates_seen = (set(), set())

    def gate_fill(role, batch):
        for cell in CELLS:
            if SLOT[role][cell][0] != batch:
                continue
            p, d, c = cell
            source = place_of(cell)
            if source not in gates_seen[role]:
                gates_seen[role].add(source)
                gate_twin((0, d, c), other).wait_recv()
                for whose in range(2):
                    row = gates[source * 2 + whose, me]
                    gate_tok[source * 2 + whose] = jnp.broadcast_to(row, (128, tok_rows)).T
            for whose in range(2):
                first = (SLOT[role][cell][1] * 2 + whose) * rows
                gate_col[pl.ds(first, rows), :] = gate_tok[source * 2 + whose, pl.ds(p * rows, rows), :]

    def compute(batch, first, last):
        if first == 0:
            ref = xs.at[pl.ds(0, PIECES)]
            remote(ref, ref, twin_send.at[0], twin_recv.at[batch], peers["twin"]).wait_recv()
            if batch == 0:
                weight_loads[0].wait()
                weight_loads[1].wait()
        if first < 4:
            hidden_part(batch, first, min(last, 4))
        if first <= 4 < last:
            by_role(lambda: gate_fill(0, batch), lambda: gate_fill(1, batch))
            if batch == 0:
                weight_loads[2].wait()
        for part in range(max(first, 4), last):
            answer_part(batch, (part - 4) * 2, (part - 3) * 2)
            sib_copy(batch, part - 4, other).start()

    def events(role, codes):
        if not codes:
            return None

        def run():
            for code in codes:
                cell = (code // 100 % 10, code // 10 % 10, code % 10)
                if code < 1000:
                    receive(role, cell)
                else:
                    send_back(role, cell)

        return run

    plans = []
    for order in ORDERS:
        plan, now = [], []
        for code in order:
            if code // 1000 == 1:
                plan.append((now, code))
                now = []
            else:
                now.append(code)
        plan.append((now, None))
        plans.append(plan)

    waiting = None
    for (end_codes, code), (mid_codes, mid_code) in zip(*plans):
        assert code == mid_code
        batch, part = (None, None) if code is None else (code // 100 % 10, code // 10 % 10)
        if waiting is not None and (end_codes or mid_codes or batch != waiting[0]):
            compute(*waiting)
            waiting = None
        by_role(events(0, end_codes), events(1, mid_codes))
        if code is not None:
            waiting = (batch, part, part + 1) if waiting is None else (batch, waiting[1], part + 1)

    def finish(role):
        sent = sum(len(moves(role, cell)) for cell in CELLS)
        ref = xs.at[pl.ds(0, sent)]
        remote(ref, ref, ag_send.at[0], ag_recv.at[0], peers["x"]).wait_send()
        sent = sum(len(moves(role, cell)) for cell in CELLS if cell[0] == 0)
        ref = gates.at[pl.ds(0, sent)]
        remote(ref, ref, gate_send.at[0], gate_recv.at[0], peers["x"]).wait_send()

    by_role(lambda: finish(0), lambda: finish(1))
    ref = xs.at[pl.ds(0, len(CELLS))]
    remote(ref, ref, twin_send.at[0], twin_recv.at[0], peers["twin"]).wait_send()
    ref = gates.at[pl.ds(0, 8)]
    remote(ref, ref, gate_send.at[1], gate_pass.at[0], peers["twin"]).wait_send()
    remote(sib, sib, sib_send.at[0], sib_recv.at[0], peers["twin"]).wait_send()
    assert put_used == [put.shape[0]] * 2
    remote(put, put, rs_send.at[0], x_recv.at[0], peers["x"]).wait_send()


def fused_scratch(n, tok_rows, width, ff):
    bf16, f32 = jnp.bfloat16, jnp.float32
    rows = tok_rows // PIECES
    chunk = (rows, width)
    buffers = [
        ((PIECES * 16,) + chunk, bf16),
        ((width, ff), bf16),
        ((width, ff), bf16),
        ((ff, width), bf16),
        ((PIECES, 8, 2) + chunk, bf16),
        ((PIECES, 8) + chunk, bf16),
        ((PIECES * 7,) + chunk, bf16),
        ((PIECES * 4,) + chunk, bf16),
        ((PIECES * 4,) + chunk, bf16),
        ((PIECES * 6,) + chunk, bf16),
        ((2 * tok_rows, ff), bf16),
        ((16, n, 1, tok_rows), f32),
        ((16, tok_rows, 128), f32),
        ((2 * tok_rows, 128), f32),
    ]
    sems = [3, PIECES, 1, PIECES * 8, 1, PIECES, 2, 8, 8, 1, PIECES, 1]
    sems += [PIECES * 4, PIECES * 4, PIECES * 6]
    size = 0
    for shape, kind in buffers:
        count = jnp.dtype(kind).itemsize
        for extent in shape:
            count = count * extent
        size = size + count
    scratch = [pltpu.VMEM(shape, kind) for shape, kind in buffers]
    return scratch + [pltpu.SemaphoreType.DMA((count,)) for count in sems], size


def fused_device(tokens, expert_ids, route_logits, w_gate, w_up, w_down):
    n = lax.axis_size("ep")
    tok_rows, width = tokens.shape
    ff = w_gate.shape[2]
    scratch, size = fused_scratch(n, tok_rows, width, ff)
    anywhere, vmem = pl.BlockSpec(memory_space=pl.ANY), pl.BlockSpec(memory_space=pltpu.VMEM)
    return pl.pallas_call(
        functools.partial(fused_kernel, n),
        out_shape=jax.ShapeDtypeStruct((tok_rows, width), jnp.bfloat16),
        in_specs=[anywhere, vmem, vmem, anywhere, anywhere, anywhere],
        out_specs=vmem,
        scratch_shapes=scratch,
        compiler_params=pltpu.CompilerParams(
            collective_id=0, has_side_effects=True, vmem_limit_bytes=VMEM_BYTES
        ),
    )(tokens, expert_ids.T, route_logits.T, w_gate, w_up, w_down)


def layer(tokens, expert_ids, route_logits, w_gate, w_up, w_down):
    n = lax.axis_size("ep")
    tok_rows, width = tokens.shape
    ff = w_gate.shape[2]
    size = fused_scratch(n, tok_rows, width, ff)[1]
    fits = size + 8 * tok_rows * width < VMEM_BYTES and width % 512 == 0 and ff % 512 == 0
    if fits and n == 16 and tok_rows == 16 * PIECES:
        return fused_device(tokens, expert_ids, route_logits, w_gate, w_up, w_down)
    return per_device(tokens, expert_ids, route_logits, w_gate, w_up, w_down)


def solution(mesh):
    in_specs = (
        P(("dp", "ep"), None),
        P(("dp", "ep"), None),
        P(("dp", "ep"), None),
        P("ep", None, None),
        P("ep", None, None),
        P("ep", None, None),
    )
    out_specs = P(("dp", "ep"), None)
    return jax.shard_map(
        layer, mesh=mesh, in_specs=in_specs, out_specs=out_specs, check_vma=False
    )
```

time: 93.7 us -> 86 us (0.918)
  Pallas kernels: 91.7 us -> 83.9 us
    pallas_call x1, Pallas kernels: 91.7 us -> 83.9 us  [fused_device(): pl.pallas_call(functools.partial(fused_kernel, n), out_shape=jax.ShapeDty...]
where the time goes in v1:
time: 86 us; the launch traced here: 85.8 us
  Pallas kernels  83.9 us (98%)
  local copies, waits for them, and re-layouts  1.88 us (2%)
    pallas_call x1, Pallas kernels, fused_device(): pl.pallas_call(functools.partial(fused_kernel, n), out_shape=jax.ShapeDty...  83.9 us
    unnamed x1, local copies, waits for them, and re-layouts  1.88 us

profile of v1, /device:TPU:0, one launch (start us, length us, event | category | flops | bytes accessed | tf_op | source)
XLA Modules:
  0.0 85.8 jit_solution(1764488348977579402)
XLA Ops:
  0.0 83.9 %shard_map.64 = bf16[128,2048]{1,0:T(8,128)(2,1)} custom-call(bf16[128,2048]{1,0:T(8,128)(2,1)} %tok_ref.1, s32[8,128]{1,0:T(8,128)} %bitcast.2, f32[8,128]{1,0:T(8,128)} %bitcast.3, bf16[1,2048,1024]{2,1,0:T(8,128)(2,1)} %wg_hbm.1, bf16[1,2048,1024]{2,1,0:T(8,128)(2,1)} %wu_hbm.1, bf16[1,1024,2048]{2,1,0:T(8,128)(2,1)} %wd_hbm.1), custom_call_target="tpu_custom_call" | custom-call | tf_op jit(solution)/shard_map/pallas_call | solution.py:545
  83.9 1.9 %copy.8 = bf16[128,2048]{1,0:T(8,128)(2,1)} copy(bf16[128,2048]{1,0:T(8,128)(2,1)} %shard_map.64) | data formatting | bytes 1048576

commit v2 on v1

--- a/solution.py
+++ b/solution.py
@@ -9,44 +9,44 @@
 
 VMEM_BYTES = 63 * 1024 * 1024
 
-KINDS = (1, 0, 0, 1, 0, 1, 0, 0)
+KINDS = (1, 0, 1, 0, 0, 1, 0, 0)
 END_BATCHES = (
-    5, 2, 0, 3, 0, 0, 0, 1, 3, 2, 7, 7, 4, 6, 2, 3,
-    7, 5, 3, 6, 1, 0, 1, 1, 6, 7, 6, 7, 6, 6, 2, 5,
-    4, 3, 1, 0, 0, 1, 3, 3, 0, 4, 2, 4, 4, 4, 1, 5,
-    5, 3, 2, 7, 7, 6, 5, 4, 1, 4, 5, 5, 7, 6, 2, 2,
+    7, 7, 1, 0, 0, 1, 1, 2, 3, 4, 6, 6, 6, 6, 5, 5,
+    7, 5, 7, 7, 6, 6, 3, 3, 2, 5, 2, 7, 5, 6, 4, 4,
+    3, 2, 0, 0, 0, 1, 2, 3, 5, 4, 4, 5, 5, 6, 2, 4,
+    7, 4, 0, 1, 3, 4, 2, 3, 3, 7, 1, 0, 0, 1, 1, 2,
 )
 MID_BATCHES = (
-    6, 6, 0, 0, 0, 1, 4, 4, 0, 2, 5, 2, 1, 2, 7, 0,
-    3, 7, 3, 1, 3, 0, 6, 6, 6, 4, 5, 5, 1, 3, 4, 6,
-    7, 1, 6, 1, 4, 2, 5, 3, 7, 5, 2, 3, 3, 2, 0, 5,
-    7, 4, 5, 4, 1, 4, 2, 2, 7, 6, 7, 5, 1, 3, 7, 0,
+    4, 2, 0, 2, 3, 3, 2, 2, 7, 4, 6, 6, 5, 4, 5, 2,
+    7, 7, 6, 6, 3, 3, 7, 1, 0, 2, 6, 6, 3, 4, 4, 4,
+    7, 6, 5, 3, 0, 2, 0, 5, 7, 7, 5, 5, 1, 3, 5, 1,
+    1, 0, 1, 7, 1, 4, 5, 1, 6, 4, 0, 0, 0, 2, 1, 3,
 )
 END_ORDER = (
-    400, 200, 0, 600, 10, 401, 700, 201, 500, 1, 410, 601, 100, 701, 20, 300,
-    420, 501, 411, 220, 101, 11, 210, 301, 430, 30, 421, 610, 221, 230, 21, 211,
-    1000, 530, 431, 1010, 1020, 730, 611, 1030, 31, 231, 1040, 1050, 130, 1100, 1110, 330,
-    1120, 2030, 2221, 2021, 731, 2411, 510, 1130, 1140, 630, 131, 2020, 1150, 2010, 1200, 110,
-    1210, 1220, 511, 2530, 2421, 1230, 520, 2231, 2031, 1240, 631, 2410, 1250, 120, 1300, 111,
-    710, 2220, 1310, 1320, 521, 2101, 2330, 1330, 2230, 2731, 531, 1340, 1350, 310, 121, 2420,
-    1400, 711, 2510, 1410, 331, 2131, 2431, 1420, 2011, 1430, 720, 2730, 1440, 1450, 620, 1500,
-    311, 2130, 2401, 1510, 320, 2521, 1520, 2430, 2631, 1530, 721, 2601, 321, 1540, 2511, 1550,
-    621, 2701, 2520, 2531, 2711, 1600, 2201, 1610, 2331, 1620, 2630, 1630, 1640, 1650, 2001, 2710,
-    1700, 1710, 2321, 2121, 2320, 2721, 1720, 1730, 2310, 2621, 1740, 2000, 2211, 1750, 2400, 2120,
-    2311, 2111, 2720, 2611, 2620, 2501, 2210, 2301, 2110, 2600, 2610, 2500, 2200, 2300, 2700, 2100,
+    700, 0, 600, 400, 701, 710, 10, 1, 500, 601, 410, 401, 610, 711, 720, 20,
+    501, 200, 411, 420, 11, 611, 300, 1000, 30, 721, 100, 1010, 1020, 730, 201, 1030,
+    421, 1040, 310, 1050, 21, 301, 31, 101, 2711, 2411, 2020, 2011, 1100, 731, 1110, 630,
+    1120, 311, 1130, 430, 1140, 530, 1150, 620, 2410, 1200, 2611, 2710, 2721, 631, 2030, 230,
+    1210, 1220, 330, 2021, 431, 1230, 621, 1240, 2421, 2010, 231, 1250, 2610, 130, 531, 1300,
+    2720, 2731, 1310, 2530, 2401, 510, 331, 1320, 1330, 2420, 110, 1340, 1350, 320, 2031, 131,
+    1400, 2730, 520, 1410, 2631, 210, 1420, 2431, 2231, 1430, 111, 1440, 120, 2230, 511, 1450,
+    321, 211, 2630, 1500, 2531, 2621, 2331, 220, 1510, 2430, 1520, 2101, 121, 521, 2510, 1530,
+    2601, 221, 1540, 1550, 2620, 1600, 1610, 2330, 2131, 2520, 2301, 1620, 1630, 2511, 1640, 1650,
+    2201, 1700, 2130, 1710, 2521, 2321, 2121, 1720, 2221, 1730, 2111, 2220, 1740, 1750, 2501, 2320,
+    2400, 2701, 2211, 2311, 2120, 2600, 2001, 2110, 2300, 2500, 2210, 2700, 2200, 2310, 2100, 2000,
 )
 MID_ORDER = (
-    0, 400, 200, 600, 430, 10, 401, 410, 30, 201, 230, 601, 210, 1, 431, 420,
-    411, 530, 730, 20, 231, 220, 31, 211, 11, 130, 421, 520, 330, 731, 630, 720,
-    221, 21, 531, 131, 120, 331, 631, 320, 721, 500, 121, 620, 100, 1000, 501, 1010,
-    621, 510, 1020, 1030, 101, 110, 1040, 1050, 700, 1100, 1110, 511, 1120, 2221, 111, 2731,
-    521, 2011, 2020, 1130, 1140, 701, 300, 1150, 2131, 1200, 321, 2010, 1210, 710, 1220, 2021,
-    1230, 610, 1240, 2401, 1250, 301, 1300, 310, 2411, 1310, 711, 2320, 1320, 2121, 1330, 611,
-    2111, 1340, 311, 1350, 2631, 1400, 1410, 2421, 1420, 2520, 2721, 2220, 1430, 1440, 2431, 1450,
-    2120, 1500, 2101, 1510, 2031, 2030, 2511, 2611, 1520, 2420, 1530, 2530, 2720, 2621, 1540, 2330,
-    2211, 1550, 2510, 2601, 1600, 2521, 1610, 2711, 2430, 1620, 2321, 2501, 1630, 2620, 1640, 2210,
-    1650, 1700, 2531, 1710, 2311, 2231, 2331, 2410, 2001, 1720, 1730, 2310, 2630, 2701, 1740, 1750,
-    2110, 2230, 2301, 2000, 2500, 2730, 2201, 2130, 2400, 2710, 2610, 2300, 2200, 2700, 2100, 2600,
+    700, 0, 400, 600, 701, 710, 30, 10, 730, 401, 410, 601, 1, 430, 711, 20,
+    31, 731, 720, 630, 411, 300, 431, 11, 530, 721, 21, 531, 631, 620, 230, 301,
+    420, 330, 1000, 520, 130, 1010, 610, 621, 1020, 231, 1030, 421, 220, 1040, 1050, 320,
+    331, 1100, 131, 1110, 120, 1120, 2711, 221, 611, 2010, 1130, 2601, 1140, 321, 521, 1150,
+    1200, 121, 500, 1210, 1220, 2631, 100, 1230, 1240, 310, 1250, 510, 1300, 1310, 200, 1320,
+    2421, 2011, 1330, 110, 101, 1340, 501, 1350, 311, 2301, 1400, 201, 2710, 2131, 1410, 210,
+    1420, 2520, 2731, 1430, 111, 2020, 511, 2411, 1440, 1450, 211, 2021, 2721, 1500, 1510, 2701,
+    1520, 2221, 2331, 1530, 2220, 2030, 1540, 2621, 1550, 2720, 2031, 2321, 1600, 2521, 2231, 1610,
+    2530, 2410, 2431, 1620, 2420, 2101, 1630, 2730, 2620, 2121, 1640, 1650, 2531, 2001, 1700, 2320,
+    1710, 2311, 2700, 2510, 1720, 2430, 2401, 1730, 2630, 2111, 1740, 2120, 1750, 2330, 2000, 2511,
+    2230, 2611, 2211, 2400, 2130, 2210, 2501, 2310, 2610, 2201, 2110, 2500, 2600, 2200, 2100, 2300,
 )
 ORDERS = (END_ORDER, MID_ORDER)
 
@@ -183,8 +183,8 @@
 def fused_kernel(
     n,
     tok_ref,
-    ids_ref,
-    logits_ref,
+    ids_hbm,
+    logits_hbm,
     wg_hbm,
     wu_hbm,
     wd_hbm,
@@ -200,6 +200,8 @@
     got_in,
     got_out,
     hid,
+    ids_ref,
+    logits_ref,
     gates,
     gate_tok,
     gate_col,
@@ -258,6 +260,13 @@
     greet("in")
     by_role(None, lambda: greet("out"))
 
+    small_loads = [
+        pltpu.make_async_copy(ids_hbm, ids_ref, load_sem.at[3]),
+        pltpu.make_async_copy(logits_hbm, logits_ref, load_sem.at[4]),
+    ]
+    for load in small_loads:
+        load.start()
+
     def chunk(role, cell, whose):
         batch, place = SLOT[role][cell]
         return xs.at[(batch * PIECES + place) * 2 + whose]
@@ -281,6 +290,8 @@
     for load in weight_loads:
         load.start()
 
+    for load in small_loads:
+        load.wait()
     logits = logits_ref[...]
     powers = jnp.exp(logits - jnp.max(logits, axis=0, keepdims=True))
     shares = powers / jnp.sum(powers, axis=0, keepdims=True)
@@ -504,7 +515,7 @@
     remote(put, put, rs_send.at[0], x_recv.at[0], peers["x"]).wait_send()
 
 
-def fused_scratch(n, tok_rows, width, ff):
+def fused_scratch(n, tok_rows, width, ff, picks):
     bf16, f32 = jnp.bfloat16, jnp.float32
     rows = tok_rows // PIECES
     chunk = (rows, width)
@@ -520,11 +531,13 @@
         ((PIECES * 4,) + chunk, bf16),
         ((PIECES * 6,) + chunk, bf16),
         ((2 * tok_rows, ff), bf16),
+        ((picks, tok_rows), jnp.int32),
+        ((picks, tok_rows), f32),
         ((16, n, 1, tok_rows), f32),
         ((16, tok_rows, 128), f32),
         ((2 * tok_rows, 128), f32),
     ]
-    sems = [3, PIECES, 1, PIECES * 8, 1, PIECES, 2, 8, 8, 1, PIECES, 1]
+    sems = [5, PIECES, 1, PIECES * 8, 1, PIECES, 2, 8, 8, 1, PIECES, 1]
     sems += [PIECES * 4, PIECES * 4, PIECES * 6]
     size = 0
     for shape, kind in buffers:
@@ -540,12 +553,12 @@
     n = lax.axis_size("ep")
     tok_rows, width = tokens.shape
     ff = w_gate.shape[2]
-    scratch, size = fused_scratch(n, tok_rows, width, ff)
+    scratch, size = fused_scratch(n, tok_rows, width, ff, expert_ids.shape[1])
     anywhere, vmem = pl.BlockSpec(memory_space=pl.ANY), pl.BlockSpec(memory_space=pltpu.VMEM)
     return pl.pallas_call(
         functools.partial(fused_kernel, n),
-        out_shape=jax.ShapeDtypeStruct((tok_rows, width), jnp.bfloat16),
-        in_specs=[anywhere, vmem, vmem, anywhere, anywhere, anywhere],
+        out_shape=pltpu.VMEM((tok_rows, width), jnp.bfloat16),
+        in_specs=[anywhere] * 6,
         out_specs=vmem,
         scratch_shapes=scratch,
         compiler_params=pltpu.CompilerParams(
@@ -558,7 +571,7 @@
     n = lax.axis_size("ep")
     tok_rows, width = tokens.shape
     ff = w_gate.shape[2]
-    size = fused_scratch(n, tok_rows, width, ff)[1]
+    size = fused_scratch(n, tok_rows, width, ff, expert_ids.shape[1])[1]
     fits = size + 8 * tok_rows * width < VMEM_BYTES and width % 512 == 0 and ff % 512 == 0
     if fits and n == 16 and tok_rows == 16 * PIECES:
         return fused_device(tokens, expert_ids, route_logits, w_gate, w_up, w_down)

time: 86 us -> 78.6 us (0.914)
  Pallas kernels: 83.9 us -> 77.7 us
  local copies, waits for them, and re-layouts: 1.88 us -> 0.8 us
    pallas_call x1, Pallas kernels: 83.9 us -> 77.7 us  [fused_device(): pl.pallas_call(functools.partial(fused_kernel, n), out_shape=pltpu.VMEM((...]
    unnamed x1, local copies, waits for them, and re-layouts: 1.88 us -> 0.8 us
where the time goes in v2:
time: 78.6 us; the launch traced here: 78.5 us
  Pallas kernels  77.7 us (99%)
  local copies, waits for them, and re-layouts  0.8 us (1%)
    pallas_call x1, Pallas kernels, fused_device(): pl.pallas_call(functools.partial(fused_kernel, n), out_shape=pltpu.VMEM((...  77.7 us

profile of v2, /device:TPU:0, one launch (start us, length us, event | category | flops | bytes accessed | tf_op | source)
XLA Modules:
  0.0 78.5 jit_solution(5205267899651674789)
XLA Ops:
  0.0 77.7 %shard_map.64 = bf16[128,2048]{1,0:T(8,128)(2,1)S(1)} custom-call(bf16[128,2048]{1,0:T(8,128)(2,1)} %tok_ref.1, s32[8,128]{1,0:T(8,128)} %bitcast.2, f32[8,128]{1,0:T(8,128)} %bitcast.3, bf16[1,2048,1024]{2,1,0:T(8,128)(2,1)} %wg_hbm.1, bf16[1,2048,1024]{2,1,0:T(8,128)(2,1)} %wu_hbm.1, bf16[1,1024,2048]{2,1,0:T(8,128)(2,1)} %wd_hbm.1), custom_call_target="tpu_custom_call" | custom-call | tf_op jit(solution)/shard_map/pallas_call | solution.py:558
  77.7 0.8 %copy.8 = bf16[128,2048]{1,0:T(8,128)(2,1)} copy(bf16[128,2048]{1,0:T(8,128)(2,1)S(1)} %shard_map.64) | data formatting | bytes 1048576

commit v3 on v2

--- a/solution.py
+++ b/solution.py
@@ -9,44 +9,50 @@
 
 VMEM_BYTES = 63 * 1024 * 1024
 
-KINDS = (1, 0, 1, 0, 0, 1, 0, 0)
+GATHER_X = (0, 0, 1, 1, 1, 1, 0, 0, 0, 0)
+SUM_Z = (1, 0, 0, 0, 0, 1, 0, 0, 1, 1)
+PARTS = (0, 1, 2, 3, 4, 4, 5, 6, 6, 7)
 END_BATCHES = (
-    7, 7, 1, 0, 0, 1, 1, 2, 3, 4, 6, 6, 6, 6, 5, 5,
-    7, 5, 7, 7, 6, 6, 3, 3, 2, 5, 2, 7, 5, 6, 4, 4,
-    3, 2, 0, 0, 0, 1, 2, 3, 5, 4, 4, 5, 5, 6, 2, 4,
-    7, 4, 0, 1, 3, 4, 2, 3, 3, 7, 1, 0, 0, 1, 1, 2,
+    1, 1, 0, 0, 0, 1, 2, 3, 0, 4, 5, 6, 4, 5, 4, 3,
+    7, 2, 6, 6, 5, 6, 3, 4, 7, 3, 7, 7, 6, 6, 6, 3,
+    5, 2, 2, 0, 0, 2, 1, 2, 7, 3, 5, 2, 5, 5, 5, 4,
+    7, 7, 0, 0, 1, 1, 4, 4, 6, 7, 1, 1, 4, 3, 2, 3,
 )
 MID_BATCHES = (
-    4, 2, 0, 2, 3, 3, 2, 2, 7, 4, 6, 6, 5, 4, 5, 2,
-    7, 7, 6, 6, 3, 3, 7, 1, 0, 2, 6, 6, 3, 4, 4, 4,
-    7, 6, 5, 3, 0, 2, 0, 5, 7, 7, 5, 5, 1, 3, 5, 1,
-    1, 0, 1, 7, 1, 4, 5, 1, 6, 4, 0, 0, 0, 2, 1, 3,
+    2, 3, 2, 1, 1, 3, 1, 5, 7, 6, 5, 5, 4, 3, 5, 2,
+    7, 6, 7, 6, 5, 3, 1, 4, 4, 5, 7, 6, 5, 4, 0, 1,
+    4, 7, 0, 0, 6, 6, 0, 2, 4, 7, 7, 3, 6, 3, 2, 2,
+    5, 1, 0, 1, 3, 2, 3, 0, 7, 0, 0, 4, 4, 2, 6, 1,
 )
 END_ORDER = (
-    700, 0, 600, 400, 701, 710, 10, 1, 500, 601, 410, 401, 610, 711, 720, 20,
-    501, 200, 411, 420, 11, 611, 300, 1000, 30, 721, 100, 1010, 1020, 730, 201, 1030,
-    421, 1040, 310, 1050, 21, 301, 31, 101, 2711, 2411, 2020, 2011, 1100, 731, 1110, 630,
-    1120, 311, 1130, 430, 1140, 530, 1150, 620, 2410, 1200, 2611, 2710, 2721, 631, 2030, 230,
-    1210, 1220, 330, 2021, 431, 1230, 621, 1240, 2421, 2010, 231, 1250, 2610, 130, 531, 1300,
-    2720, 2731, 1310, 2530, 2401, 510, 331, 1320, 1330, 2420, 110, 1340, 1350, 320, 2031, 131,
-    1400, 2730, 520, 1410, 2631, 210, 1420, 2431, 2231, 1430, 111, 1440, 120, 2230, 511, 1450,
-    321, 211, 2630, 1500, 2531, 2621, 2331, 220, 1510, 2430, 1520, 2101, 121, 521, 2510, 1530,
-    2601, 221, 1540, 1550, 2620, 1600, 1610, 2330, 2131, 2520, 2301, 1620, 1630, 2511, 1640, 1650,
-    2201, 1700, 2130, 1710, 2521, 2321, 2121, 1720, 2221, 1730, 2111, 2220, 1740, 1750, 2501, 2320,
-    2400, 2701, 2211, 2311, 2120, 2600, 2001, 2110, 2300, 2500, 2210, 2700, 2200, 2310, 2100, 2000,
+    500, 0, 400, 800, 900, 510, 501, 700, 1, 10, 410, 401, 100, 801, 710, 901,
+    810, 701, 910, 520, 420, 11, 300, 101, 20, 511, 711, 811, 820, 411, 200, 911,
+    530, 10000, 720, 10010, 301, 600, 10020, 21, 430, 10030, 521, 30, 821, 10040, 421, 10050,
+    531, 201, 431, 721, 830, 20520, 601, 20411, 20511, 20711, 20020, 10100, 920, 10110, 31, 20810,
+    20010, 610, 10120, 831, 10130, 930, 20011, 10140, 730, 10150, 921, 20710, 20811, 230, 611, 20530,
+    130, 20021, 20721, 10200, 931, 331, 20821, 731, 10210, 20911, 10220, 630, 20820, 10230, 620, 131,
+    20910, 10240, 10250, 110, 20720, 10300, 10310, 631, 20510, 20030, 20201, 20421, 231, 10320, 210, 20930,
+    621, 20611, 10330, 10340, 120, 111, 20531, 20521, 10350, 310, 20431, 20410, 20401, 10400, 220, 20420,
+    10410, 20131, 20031, 20921, 20331, 211, 10420, 10430, 121, 330, 20301, 20931, 10440, 10450, 311, 20430,
+    20601, 10500, 320, 10510, 20130, 20830, 20731, 20231, 10520, 221, 20831, 10530, 20631, 20920, 321, 10540,
+    20101, 10550, 10600, 20730, 10610, 10620, 20230, 20121, 20621, 20610, 10630, 10640, 20630, 10650, 20001, 10700,
+    10710, 20330, 20221, 20120, 20321, 10720, 10730, 20620, 20111, 10740, 20100, 20000, 10750, 20211, 20220, 20311,
+    20320, 20901, 20110, 20701, 20501, 20210, 20801, 20200, 20310, 20600, 20900, 20300, 20700, 20500, 20400, 20800,
 )
 MID_ORDER = (
-    700, 0, 400, 600, 701, 710, 30, 10, 730, 401, 410, 601, 1, 430, 711, 20,
-    31, 731, 720, 630, 411, 300, 431, 11, 530, 721, 21, 531, 631, 620, 230, 301,
-    420, 330, 1000, 520, 130, 1010, 610, 621, 1020, 231, 1030, 421, 220, 1040, 1050, 320,
-    331, 1100, 131, 1110, 120, 1120, 2711, 221, 611, 2010, 1130, 2601, 1140, 321, 521, 1150,
-    1200, 121, 500, 1210, 1220, 2631, 100, 1230, 1240, 310, 1250, 510, 1300, 1310, 200, 1320,
-    2421, 2011, 1330, 110, 101, 1340, 501, 1350, 311, 2301, 1400, 201, 2710, 2131, 1410, 210,
-    1420, 2520, 2731, 1430, 111, 2020, 511, 2411, 1440, 1450, 211, 2021, 2721, 1500, 1510, 2701,
-    1520, 2221, 2331, 1530, 2220, 2030, 1540, 2621, 1550, 2720, 2031, 2321, 1600, 2521, 2231, 1610,
-    2530, 2410, 2431, 1620, 2420, 2101, 1630, 2730, 2620, 2121, 1640, 1650, 2531, 2001, 1700, 2320,
-    1710, 2311, 2700, 2510, 1720, 2430, 2401, 1730, 2630, 2111, 1740, 2120, 1750, 2330, 2000, 2511,
-    2230, 2611, 2211, 2400, 2130, 2210, 2501, 2310, 2610, 2201, 2110, 2500, 2600, 2200, 2100, 2300,
+    500, 0, 400, 800, 700, 900, 510, 530, 1, 30, 410, 10, 801, 430, 701, 501,
+    810, 830, 901, 401, 520, 531, 31, 431, 710, 20, 730, 11, 930, 811, 420, 831,
+    511, 130, 711, 411, 521, 330, 21, 421, 731, 820, 910, 931, 230, 10000, 600, 131,
+    10010, 821, 920, 10020, 331, 10030, 720, 630, 911, 10040, 220, 10050, 601, 120, 10100, 921,
+    231, 10110, 321, 721, 20731, 20510, 20411, 10120, 620, 10130, 631, 10140, 610, 121, 10150, 10200,
+    100, 10210, 10220, 20331, 20701, 221, 621, 10230, 200, 611, 10240, 10250, 101, 110, 20011, 10300,
+    300, 10310, 20010, 10320, 20131, 210, 10330, 20811, 20721, 201, 10340, 20711, 10350, 320, 20631, 111,
+    20810, 10400, 20431, 301, 10410, 20001, 20020, 10420, 310, 10430, 20710, 20121, 10440, 20621, 20511, 211,
+    10450, 10500, 311, 20221, 20410, 10510, 20030, 20021, 20231, 20000, 20920, 10520, 10530, 20611, 20911, 10540,
+    10550, 20921, 20321, 10600, 20801, 10610, 20301, 20031, 20700, 20120, 10620, 20820, 10630, 20901, 20821, 10640,
+    20111, 20910, 20931, 10650, 20800, 20720, 10700, 20130, 10710, 20101, 20421, 20520, 20521, 20220, 20930, 20830,
+    20201, 10720, 20831, 10730, 20211, 10740, 20730, 20620, 10750, 20531, 20530, 20311, 20320, 20420, 20601, 20230,
+    20900, 20110, 20501, 20401, 20630, 20610, 20330, 20210, 20430, 20310, 20500, 20100, 20400, 20600, 20200, 20300,
 )
 ORDERS = (END_ORDER, MID_ORDER)
 
@@ -135,15 +141,18 @@
     )
 
 
-PIECES = len(KINDS)
-CELLS = [(p, d, c) for p in range(PIECES) for d in range(4) for c in range(2)]
-PARTS = 6
+SENDS = len(GATHER_X)
+PIECES = len(END_BATCHES) // 8
+CELLS = [(h, d, c) for h in range(SENDS) for d in range(4) for c in range(2)]
 
 
 def slots_of(batches):
     filled, table = [0] * PIECES, {}
-    for cell, batch in zip(CELLS, batches):
-        table[cell] = (batch, filled[batch])
+    places = [(piece, d, c) for piece in range(PIECES) for d in range(4) for c in range(2)]
+    for (piece, d, c), batch in zip(places, batches):
+        for p in range(SENDS):
+            if PARTS[p] == piece:
+                table[p, d, c] = (batch, filled[batch])
         filled[batch] += 1
     return table
 
@@ -161,7 +170,7 @@
 
 def moves(role, cell):
     p, d, c = cell
-    first_z = KINDS[p] == 0
+    first_z = not GATHER_X[p]
     out = []
     if d == 0 and (c == 0 or not first_z):
         if role == 0:
@@ -224,6 +233,8 @@
     tok_rows, width = tok_ref.shape
     rows = tok_rows // PIECES
     ff = wg.shape[1]
+    ff_tile = ff // 4
+    out_tile = width // 4
     me = lax.axis_index("ep")
     core, chip = me % 2, me // 2
     other = 1 - core
@@ -233,9 +244,9 @@
     at_end = jnp.logical_or(z == 0, z == depth - 1)
     at_mid = jnp.logical_not(at_end)
     peers = {
-        "in": ((z + inward) * 2 + x) * 2 + core,
-        "out": ((z - inward) * 2 + x) * 2 + core,
-        "x": (z * 2 + 1 - x) * 2 + core,
+        "in": ((z + inward) * 2 + x) * 2 + other,
+        "out": ((z - inward) * 2 + x) * 2 + other,
+        "x": (z * 2 + 1 - x) * 2 + other,
         "twin": chip * 2 + other,
     }
 
@@ -267,18 +278,25 @@
     for load in small_loads:
         load.start()
 
+    def cols_of(cell):
+        piece = PARTS[cell[0]]
+        part_width = width // PARTS.count(piece)
+        return pl.ds((cell[0] - PARTS.index(piece)) * part_width, part_width)
+
     def chunk(role, cell, whose):
         batch, place = SLOT[role][cell]
-        return xs.at[(batch * PIECES + place) * 2 + whose]
+        return xs.at[(batch * PIECES + place) * 2 + whose, :, cols_of(cell)]
 
     def own_load(role, p):
         return pltpu.make_async_copy(
-            tok_ref.at[pl.ds(p * rows, rows)], chunk(role, (p, 0, 0), core), tok_sem.at[p]
+            tok_ref.at[pl.ds(PARTS[p] * rows, rows), cols_of((p, 0, 0))],
+            chunk(role, (p, 0, 0), core),
+            tok_sem.at[p],
         )
 
     def load_all(role):
         for code in ORDERS[role]:
-            if code // 1000 == 0 and code % 100 == 0:
+            if code // 10000 == 0 and code % 100 == 0:
                 own_load(role, code // 100).start()
 
     by_role(lambda: load_all(0), lambda: load_all(1))
@@ -290,23 +308,24 @@
     for load in weight_loads:
         load.start()
 
-    for load in small_loads:
-        load.wait()
-    logits = logits_ref[...]
-    powers = jnp.exp(logits - jnp.max(logits, axis=0, keepdims=True))
-    shares = powers / jnp.sum(powers, axis=0, keepdims=True)
-    ids = ids_ref[...]
-    for expert in range(n):
-        gates[core, expert] = jnp.sum(
-            jnp.where(ids == expert, shares, 0.0), axis=0, keepdims=True
-        )
+    def own_gates():
+        for load in small_loads:
+            load.wait()
+        logits = logits_ref[...]
+        powers = jnp.exp(logits - jnp.max(logits, axis=0, keepdims=True))
+        shares = powers / jnp.sum(powers, axis=0, keepdims=True)
+        ids = ids_ref[...]
+        for expert in range(n):
+            gates[core, expert] = jnp.sum(
+                jnp.where(ids == expert, shares, 0.0), axis=0, keepdims=True
+            )
 
     by_role(lambda: pl.semaphore_wait(barrier, 3), lambda: pl.semaphore_wait(barrier, 4))
 
     def ag_copy(role, cell, link, to_role, to_cell):
         return remote(
             chunk(role, cell, core),
-            chunk(to_role, to_cell, core),
+            chunk(to_role, to_cell, other),
             ag_send.at[0],
             ag_recv.at[at(to_cell)],
             peers[link],
@@ -320,7 +339,7 @@
     def gate_copy(cell, link, to_cell):
         return remote(
             gates.at[place_of(cell) * 2 + core],
-            gates.at[place_of(to_cell) * 2 + core],
+            gates.at[place_of(to_cell) * 2 + other],
             gate_send.at[0],
             gate_recv.at[place_of(to_cell)],
             peers[link],
@@ -335,6 +354,8 @@
         p, d, c = cell
         lead = p == 0
         if (d, c) == (0, 0):
+            if lead:
+                own_gates()
             own_load(role, p).wait()
         else:
             if lead:
@@ -348,8 +369,8 @@
             gate_twin(cell, core).start()
         pass_copy(role, cell, core).start()
 
-    def sib_copy(batch, half, whose):
-        cols = pl.ds(half * (width // 2), width // 2)
+    def sib_copy(batch, part, whose):
+        cols = pl.ds(pl.multiple_of(part * out_tile, out_tile), out_tile)
         return remote(
             ps.at[batch, :, whose, :, cols],
             sib.at[batch, :, :, cols],
@@ -363,13 +384,15 @@
 
     def send_back(role, cell):
         p, d, c = cell
-        first_z = KINDS[p] == 0
+        first_z = not SUM_Z[p]
         batch, place = SLOT[role][cell]
+        cols = cols_of(cell)
         if batch not in sib_seen[role]:
             sib_seen[role].add(batch)
             ref = sib.at[batch]
             remote(ref, ref, sib_send.at[0], sib_recv.at[batch], peers["twin"]).wait_recv()
-        total = ps[batch, place, core].astype(jnp.float32) + sib[batch, place].astype(jnp.float32)
+        total = ps[batch, place, core, :, cols].astype(jnp.float32)
+        total = total + sib[batch, place, :, cols].astype(jnp.float32)
         inbox = []
         if c == 0 and (first_z or d == 0):
             inbox.append((got_x, x_recv, p * 4 + d))
@@ -379,14 +402,14 @@
             if role == 1 and d < 3:
                 inbox.append((got_out, out_recv, (p * 3 + d) * 2 + c))
         for buffer, sem, index in inbox:
-            ref = buffer.at[index]
+            ref = buffer.at[index, :, pl.ds(0, cols.size)]
             remote(ref, ref, rs_send.at[0], sem.at[index], peers["x"]).wait_recv()
-            total = total + buffer[index].astype(jnp.float32)
+            total = total + buffer[index, :, pl.ds(0, cols.size)].astype(jnp.float32)
         total = total.astype(jnp.bfloat16)
         if c == 1 and (first_z or d == 0):
             link, buffer, sem, index = "x", got_x, x_recv, p * 4 + d
         elif d == 0:
-            out_ref[pl.ds(p * rows, rows), :] = total
+            out_ref[pl.ds(PARTS[p] * rows, rows), cols] = total
             return
         elif role == 0:
             link, buffer, sem, index = "in", got_out, out_recv, (p * 3 + d - 1) * 2 + c
@@ -396,11 +419,15 @@
             link, buffer, sem, index = "in", got_in, in_recv, (p * 2 + d - 1) * 2 + c
         slot = put_used[role]
         put_used[role] += 1
-        put[slot] = total
-        remote(put.at[slot], buffer.at[index], rs_send.at[0], sem.at[index], peers[link]).start()
-
-    ff_tile = ff // 4
-    out_tile = width // 4
+        used = pl.ds(0, cols.size)
+        put[slot, :, used] = total
+        remote(
+            put.at[slot, :, used],
+            buffer.at[index, :, used],
+            rs_send.at[0],
+            sem.at[index],
+            peers[link],
+        ).start()
 
     def hidden_part(batch, first, last):
         def body(j, carry):
@@ -421,6 +448,7 @@
             ps[batch, :, :, :, cols] = (
                 (answer * scale).astype(jnp.bfloat16).reshape(PIECES, 2, rows, out_tile)
             )
+            sib_copy(batch, j, other).start()
             return carry
 
         lax.fori_loop(first, last, body, 0)
@@ -429,9 +457,9 @@
 
     def gate_fill(role, batch):
         for cell in CELLS:
-            if SLOT[role][cell][0] != batch:
+            p, d, c = cell
+            if SLOT[role][cell][0] != batch or PARTS.index(PARTS[p]) != p:
                 continue
-            p, d, c = cell
             source = place_of(cell)
             if source not in gates_seen[role]:
                 gates_seen[role].add(source)
@@ -441,7 +469,9 @@
                     gate_tok[source * 2 + whose] = jnp.broadcast_to(row, (128, tok_rows)).T
             for whose in range(2):
                 first = (SLOT[role][cell][1] * 2 + whose) * rows
-                gate_col[pl.ds(first, rows), :] = gate_tok[source * 2 + whose, pl.ds(p * rows, rows), :]
+                gate_col[pl.ds(first, rows), :] = gate_tok[
+                    source * 2 + whose, pl.ds(PARTS[p] * rows, rows), :
+                ]
 
     def compute(batch, first, last):
         if first == 0:
@@ -456,9 +486,8 @@
             by_role(lambda: gate_fill(0, batch), lambda: gate_fill(1, batch))
             if batch == 0:
                 weight_loads[2].wait()
-        for part in range(max(first, 4), last):
-            answer_part(batch, (part - 4) * 2, (part - 3) * 2)
-            sib_copy(batch, part - 4, other).start()
+        if last > 4:
+            answer_part(batch, max(first, 4) * 2 - 8, last * 2 - 8)
 
     def events(role, codes):
         if not codes:
@@ -466,8 +495,8 @@
 
         def run():
             for code in codes:
-                cell = (code // 100 % 10, code // 10 % 10, code % 10)
-                if code < 1000:
+                cell = (code // 100 % 100, code // 10 % 10, code % 10)
+                if code < 10000:
                     receive(role, cell)
                 else:
                     send_back(role, cell)
@@ -478,7 +507,7 @@
     for order in ORDERS:
         plan, now = [], []
         for code in order:
-            if code // 1000 == 1:
+            if code // 10000 == 1:
                 plan.append((now, code))
                 now = []
             else:
@@ -489,7 +518,7 @@
     waiting = None
     for (end_codes, code), (mid_codes, mid_code) in zip(*plans):
         assert code == mid_code
-        batch, part = (None, None) if code is None else (code // 100 % 10, code // 10 % 10)
+        batch, part = (None, None) if code is None else (code // 100 % 100, code // 10 % 10)
         if waiting is not None and (end_codes or mid_codes or batch != waiting[0]):
             compute(*waiting)
             waiting = None
@@ -498,21 +527,22 @@
             waiting = (batch, part, part + 1) if waiting is None else (batch, waiting[1], part + 1)
 
     def finish(role):
-        sent = sum(len(moves(role, cell)) for cell in CELLS)
-        ref = xs.at[pl.ds(0, sent)]
+        sent = sum(len(moves(role, cell)) * 2 // PARTS.count(PARTS[cell[0]]) for cell in CELLS)
+        ref = xs.at[pl.ds(0, sent // 2)]
         remote(ref, ref, ag_send.at[0], ag_recv.at[0], peers["x"]).wait_send()
         sent = sum(len(moves(role, cell)) for cell in CELLS if cell[0] == 0)
         ref = gates.at[pl.ds(0, sent)]
         remote(ref, ref, gate_send.at[0], gate_recv.at[0], peers["x"]).wait_send()
 
     by_role(lambda: finish(0), lambda: finish(1))
-    ref = xs.at[pl.ds(0, len(CELLS))]
+    ref = xs.at[pl.ds(0, len(END_BATCHES))]
     remote(ref, ref, twin_send.at[0], twin_recv.at[0], peers["twin"]).wait_send()
     ref = gates.at[pl.ds(0, 8)]
     remote(ref, ref, gate_send.at[1], gate_pass.at[0], peers["twin"]).wait_send()
     remote(sib, sib, sib_send.at[0], sib_recv.at[0], peers["twin"]).wait_send()
-    assert put_used == [put.shape[0]] * 2
-    remote(put, put, rs_send.at[0], x_recv.at[0], peers["x"]).wait_send()
+    assert put_used == [SENDS * 7] * 2
+    ref = put.at[pl.ds(0, PIECES * 7)]
+    remote(ref, ref, rs_send.at[0], x_recv.at[0], peers["x"]).wait_send()
 
 
 def fused_scratch(n, tok_rows, width, ff, picks):
@@ -526,10 +556,10 @@
         ((ff, width), bf16),
         ((PIECES, 8, 2) + chunk, bf16),
         ((PIECES, 8) + chunk, bf16),
-        ((PIECES * 7,) + chunk, bf16),
-        ((PIECES * 4,) + chunk, bf16),
-        ((PIECES * 4,) + chunk, bf16),
-        ((PIECES * 6,) + chunk, bf16),
+        ((SENDS * 7,) + chunk, bf16),
+        ((SENDS * 4,) + chunk, bf16),
+        ((SENDS * 4,) + chunk, bf16),
+        ((SENDS * 6,) + chunk, bf16),
         ((2 * tok_rows, ff), bf16),
         ((picks, tok_rows), jnp.int32),
         ((picks, tok_rows), f32),
@@ -537,8 +567,8 @@
         ((16, tok_rows, 128), f32),
         ((2 * tok_rows, 128), f32),
     ]
-    sems = [5, PIECES, 1, PIECES * 8, 1, PIECES, 2, 8, 8, 1, PIECES, 1]
-    sems += [PIECES * 4, PIECES * 4, PIECES * 6]
+    sems = [5, SENDS, 1, SENDS * 8, 1, PIECES, 2, 8, 8, 1, PIECES, 1]
+    sems += [SENDS * 4, SENDS * 4, SENDS * 6]
     size = 0
     for shape, kind in buffers:
         count = jnp.dtype(kind).itemsize

time: 78.6 us -> 76.8 us (0.977)
  Pallas kernels: 77.7 us -> 75.9 us
    pallas_call x1, Pallas kernels: 77.7 us -> 75.9 us  [fused_device(): pl.pallas_call(functools.partial(fused_kernel, n), out_shape=pltpu.VMEM((...]
where the time goes in v3:
time: 76.8 us; the launch traced here: 76.7 us
  Pallas kernels  75.9 us (99%)
  local copies, waits for them, and re-layouts  0.8 us (1%)
    pallas_call x1, Pallas kernels, fused_device(): pl.pallas_call(functools.partial(fused_kernel, n), out_shape=pltpu.VMEM((...  75.9 us

profile of v3, /device:TPU:0, one launch (start us, length us, event | category | flops | bytes accessed | tf_op | source)
XLA Modules:
  0.0 76.7 jit_solution(6125261704644767857)
XLA Ops:
  0.0 75.9 %shard_map.64 = bf16[128,2048]{1,0:T(8,128)(2,1)S(1)} custom-call(bf16[128,2048]{1,0:T(8,128)(2,1)} %tok_ref.1, s32[8,128]{1,0:T(8,128)} %bitcast.2, f32[8,128]{1,0:T(8,128)} %bitcast.3, bf16[1,2048,1024]{2,1,0:T(8,128)(2,1)} %wg_hbm.1, bf16[1,2048,1024]{2,1,0:T(8,128)(2,1)} %wu_hbm.1, bf16[1,1024,2048]{2,1,0:T(8,128)(2,1)} %wd_hbm.1), custom_call_target="tpu_custom_call" | custom-call | tf_op jit(solution)/shard_map/pallas_call | solution.py:588
  75.9 0.8 %copy.8 = bf16[128,2048]{1,0:T(8,128)(2,1)} copy(bf16[128,2048]{1,0:T(8,128)(2,1)S(1)} %shard_map.64) | data formatting | bytes 1048576

commit v4 on v3

--- a/solution.py
+++ b/solution.py
@@ -234,7 +234,7 @@
     rows = tok_rows // PIECES
     ff = wg.shape[1]
     ff_tile = ff // 4
-    out_tile = width // 4
+    out_tile = width // 2
     me = lax.axis_index("ep")
     core, chip = me % 2, me // 2
     other = 1 - core
@@ -305,8 +305,6 @@
         pltpu.make_async_copy(wu_hbm.at[0], wu, load_sem.at[1]),
         pltpu.make_async_copy(wd_hbm.at[0], wd, load_sem.at[2]),
     ]
-    for load in weight_loads:
-        load.start()
 
     def own_gates():
         for load in small_loads:
@@ -316,11 +314,13 @@
         shares = powers / jnp.sum(powers, axis=0, keepdims=True)
         ids = ids_ref[...]
         for expert in range(n):
-            gates[core, expert] = jnp.sum(
+            gates[core, pl.ds(expert, 1), :] = jnp.sum(
                 jnp.where(ids == expert, shares, 0.0), axis=0, keepdims=True
             )
 
     by_role(lambda: pl.semaphore_wait(barrier, 3), lambda: pl.semaphore_wait(barrier, 4))
+    for load in weight_loads:
+        load.start()
 
     def ag_copy(role, cell, link, to_role, to_cell):
         return remote(
@@ -465,7 +465,7 @@
                 gates_seen[role].add(source)
                 gate_twin((0, d, c), other).wait_recv()
                 for whose in range(2):
-                    row = gates[source * 2 + whose, me]
+                    row = gates[source * 2 + whose, pl.ds(me, 1), :]
                     gate_tok[source * 2 + whose] = jnp.broadcast_to(row, (128, tok_rows)).T
             for whose in range(2):
                 first = (SLOT[role][cell][1] * 2 + whose) * rows
@@ -487,7 +487,7 @@
             if batch == 0:
                 weight_loads[2].wait()
         if last > 4:
-            answer_part(batch, max(first, 4) * 2 - 8, last * 2 - 8)
+            answer_part(batch, max(first, 4) - 4, last - 4)
 
     def events(role, codes):
         if not codes:
@@ -563,7 +563,7 @@
         ((2 * tok_rows, ff), bf16),
         ((picks, tok_rows), jnp.int32),
         ((picks, tok_rows), f32),
-        ((16, n, 1, tok_rows), f32),
+        ((16, n, tok_rows), f32),
         ((16, tok_rows, 128), f32),
         ((2 * tok_rows, 128), f32),
     ]

time: 76.8 us -> 76.6 us (level)
  no operation moved by 1% of the time
where the time goes in v4:
time: 76.6 us; the launch traced here: 76.5 us
  Pallas kernels  75.7 us (99%)
  local copies, waits for them, and re-layouts  0.8 us (1%)
    pallas_call x1, Pallas kernels, fused_device(): pl.pallas_call(functools.partial(fused_kernel, n), out_shape=pltpu.VMEM((...  75.7 us

profile of v4, /device:TPU:0, one launch (start us, length us, event | category | flops | bytes accessed | tf_op | source)
XLA Modules:
  0.0 76.5 jit_solution(4349138987679161549)
XLA Ops:
  0.0 75.7 %shard_map.64 = bf16[128,2048]{1,0:T(8,128)(2,1)S(1)} custom-call(bf16[128,2048]{1,0:T(8,128)(2,1)} %tok_ref.1, s32[8,128]{1,0:T(8,128)} %bitcast.2, f32[8,128]{1,0:T(8,128)} %bitcast.3, bf16[1,2048,1024]{2,1,0:T(8,128)(2,1)} %wg_hbm.1, bf16[1,2048,1024]{2,1,0:T(8,128)(2,1)} %wu_hbm.1, bf16[1,1024,2048]{2,1,0:T(8,128)(2,1)} %wd_hbm.1), custom_call_target="tpu_custom_call" | custom-call | tf_op jit(solution)/shard_map/pallas_call | solution.py:588
  75.7 0.8 %copy.8 = bf16[128,2048]{1,0:T(8,128)(2,1)} copy(bf16[128,2048]{1,0:T(8,128)(2,1)S(1)} %shard_map.64) | data formatting | bytes 1048576
